TPU v7x, 32 devices: a whole 2x2x4 slice. The times are simulated.
32 devices in a mesh: dp: 2 (over y), expert: 4 (over z), tile: 4 (over x, core).
Axes of the slice: x: 2, y: 2, z: 4, core: 2. Of those that a mesh axis runs over, the one named last changes fastest.
Arguments:
- tokens: bfloat16 [512, 4096], P(('dp', 'expert'), 'tile'), may hold values from -6 to 6
- hidden: bfloat16 [512, 2, 7168], P(('dp', 'expert'), None, 'tile'), may hold values from -6 to 6
- routes: int32 [512, 2], P(('dp', 'expert')), may hold values from 0 to 3, all different within a row; in each aligned block of 64 rows (0 to 63, 64 to 127, ...) at most 40 rows name the same one
- lengths: int32 [8], P(('dp', 'expert')), may hold values from 1 to 64, as said below
Outputs:
- hessian_in: float32 [4, 4096, 4096], P('expert', 'tile', 'dp')
- hessian_down: float32 [4, 7168, 7168], P('expert', 'tile', 'dp')
Inputs may be any that keep to these rules, and one draw needn't show every extreme that they name: `routes`: in each aligned block of 64 rows (the rows of one group) no expert is named by more than 40 rows, a bound that some block reaches. The live rows of group g are its first lengths[g] rows; the last group is full.
All inputs are finite; a program needn't handle non-finite values.
Results may differ from a plain program's by a relative error of at most 0.0003.
Values may be sent and summed in bfloat16 or wider, within the bound.
No kernel may reach another device: no remote copies, remote signals or barrier semaphores. Data moves between devices by JAX's collectives and lax.ppermute only.
A program may use at most 128 MiB of HBM per device.

v0:
```python
import jax
import jax.numpy as jnp
from jax import lax
from jax.sharding import PartitionSpec as P


def broadcast(value, axis, source):
    kept = jnp.where(lax.axis_index(axis) == source, value, 0).astype(value.dtype)
    return lax.psum(kept, axis)


def contract(left, right):
    return lax.dot_general(
        left, right, (((0,), (0,)), ((), ())), preferred_element_type=jnp.float32
    )


def dispatch_tables(routes, live_count, experts, share_size, senders):
    token_count = routes.shape[0]
    top_count = routes.shape[1]
    flat_routes = routes.reshape(token_count * top_count)
    pair_index = jnp.arange(token_count * top_count, dtype=jnp.int32)
    pair_live = pair_index // top_count < live_count
    expert_ids = jnp.arange(experts, dtype=jnp.int32)
    onehot = ((flat_routes[:, None] == expert_ids[None, :]) & pair_live[:, None]).astype(
        jnp.float32
    )
    before = jnp.cumsum(onehot, axis=0) - onehot
    position = jnp.sum(before * onehot, axis=1).astype(jnp.int32)
    target = (
        position // share_size * (experts * share_size)
        + flat_routes * share_size
        + position % share_size
    )
    slot_total = senders * experts * share_size
    placed = (target[None, :] == jnp.arange(slot_total, dtype=jnp.int32)[:, None]) & pair_live[
        None, :
    ]
    return (placed.astype(jnp.float32), jnp.sum(onehot, axis=0))


def on_device(tokens, hidden, routes, lengths):
    experts = lax.axis_size("expert")
    senders = lax.axis_size("dp")
    tiles = lax.axis_size("tile")
    token_count = tokens.shape[0]
    top_count = routes.shape[1]
    share_size = (5 * token_count + 2 * experts * senders - 1) // (2 * experts * senders)
    placed, local_counts = dispatch_tables(routes, lengths[0], experts, share_size, senders)
    slot_total = placed.shape[0]
    by_token = jnp.sum(placed.reshape(slot_total, token_count, top_count), axis=2).astype(
        jnp.bfloat16
    )
    send_tokens = jnp.dot(by_token, tokens, preferred_element_type=jnp.float32).astype(jnp.bfloat16)
    flat_hidden = hidden.reshape(token_count * top_count, hidden.shape[2])
    send_hidden = jnp.dot(
        placed.astype(jnp.bfloat16), flat_hidden, preferred_element_type=jnp.float32
    ).astype(jnp.bfloat16)
    slot_tokens, slot_hidden = (
        lax.all_to_all(send_tokens, ("dp", "expert"), split_axis=0, concat_axis=0, tiled=True),
        lax.all_to_all(send_hidden, ("dp", "expert"), split_axis=0, concat_axis=0, tiled=True),
    )
    global_counts = lax.psum(local_counts, ("dp", "expert"))
    own_expert = lax.axis_index("expert")
    own_count = jnp.sum(
        jnp.where(jnp.arange(experts, dtype=jnp.int32) == own_expert, global_counts, 0.0)
    )
    factor = 2.0 / jnp.maximum(own_count, 1.0)
    all_tokens, all_hidden = (
        lax.all_gather(slot_tokens, "dp", axis=0, tiled=True),
        lax.all_gather(slot_hidden, "dp", axis=0, tiled=True),
    )
    width_tokens = slot_tokens.shape[1] * tiles // senders
    width_hidden = slot_hidden.shape[1] * tiles // senders
    group_index = lax.axis_index("dp")
    if senders % tiles == 0:
        source_tile = group_index * tiles // senders
        offset_tokens = group_index * width_tokens - source_tile * slot_tokens.shape[1]
        offset_hidden = group_index * width_hidden - source_tile * slot_hidden.shape[1]
        own_tokens = lax.dynamic_slice_in_dim(all_tokens, offset_tokens, width_tokens, 1)
        own_hidden = lax.dynamic_slice_in_dim(all_hidden, offset_hidden, width_hidden, 1)
        joined = jnp.concatenate([own_tokens, own_hidden], axis=1)
        arrived = broadcast(joined, "tile", source_tile)
        column_tokens = arrived[:, :width_tokens]
        column_hidden = arrived[:, width_tokens:]
    else:
        wide_tokens, wide_hidden = (
            lax.all_gather(all_tokens, "tile", axis=1, tiled=True),
            lax.all_gather(all_hidden, "tile", axis=1, tiled=True),
        )
        column_tokens = lax.dynamic_slice_in_dim(
            wide_tokens, group_index * width_tokens, width_tokens, 1
        )
        column_hidden = lax.dynamic_slice_in_dim(
            wide_hidden, group_index * width_hidden, width_hidden, 1
        )
    gram_tokens = contract(all_tokens, column_tokens)
    gram_hidden = contract(all_hidden, column_hidden)
    return ((gram_tokens * factor)[None], (gram_hidden * factor)[None])


def solution(mesh):
    placed = (
        P(("dp", "expert"), "tile"),
        P(("dp", "expert"), None, "tile"),
        P(("dp", "expert"), None),
        P(("dp", "expert")),
    )
    return jax.shard_map(
        on_device,
        mesh=mesh,
        in_specs=placed,
        out_specs=(P("expert", "tile", "dp"), P("expert", "tile", "dp")),
        check_vma=False,
    )
```

profile of v0, /device:TPU:0, one launch (start us, length us, event | category | flops | bytes accessed | tf_op | source)
XLA Modules:
  0.0 152.8 jit_solution(17547992000557333005)
XLA Ops:
  7.2 0.0 copy-start
  7.2 0.0 copy-start.2
  7.9 0.8 copy.20
  8.7 0.1 eq.43
  8.8 0.1 fusion.5
  8.9 0.2 reduce_window_sum.11
  9.1 0.2 fusion.6
  9.3 1.2 reshape.90
  10.5 0.3 convolution_convert_fusion
  10.8 1.0 all_to_all.19
  11.8 7.3 %all-to-all-start.1 = ((bf16[8,20,1792]{2,1,0:T(8,128)(2,1)}), bf16[8,20,1792]{2,1,0:T(8,128)(2,1)S(1)}, u32[]{:S(2)}, u32[]{:S(2)}) async-start(bf16[8,20,1792]{2,1,0:T(8,128)(2,1)} %all_to_all.19), calls=%async_computation.1 | async-start | bytes 1376256 | tf_op jit(solution)/shard_map/all_to_all | solution.py:61
  19.1 0.0 all-gather.6.cloned.1.call-start
  19.1 0.1 ne.82
  19.3 0.1 copy.22
  19.4 0.1 div.25
  19.5 0.1 copy.23
  19.6 0.1 rem.32
  19.8 0.1 copy.21
  19.8 0.0 copy-done.2
  19.9 18.1 %all-to-all-done.1 = bf16[8,20,1792]{2,1,0:T(8,128)(2,1)S(1)} async-done(((bf16[8,20,1792]{2,1,0:T(8,128)(2,1)}), bf16[8,20,1792]{2,1,0:T(8,128)(2,1)S(1)}, u32[]{:S(2)}, u32[]{:S(2)}) %all-to-all-start.1) | async-done | bytes 573472 | tf_op jit(solution)/shard_map/all_to_all | solution.py:61
  38.0 0.9 all_to_all.21
  38.9 0.0 all-gather.6.cloned.1.call-update
  38.9 0.0 all-gather.4.cloned.1.call-start
  39.0 0.1 convert_reduce_fusion
  39.1 0.0 copy-done
  39.1 0.3 convolution_convert_fusion.1
  39.4 0.1 all_to_all.16
  39.5 14.5 %all_to_all.24 = bf16[8,20,1024]{2,1,0:T(8,128)(2,1)S(1)} all-to-all(bf16[8,20,1024]{2,1,0:T(8,128)(2,1)S(1)} %all_to_all.16), channel_id=1, replica_groups=mesh['dp'=2,'expert'=4,'tile'=4] {'dp','expert'}, dimensions={0} | all-to-all | bytes 655360 | tf_op jit(solution)/shard_map/all_to_all | solution.py:60
  54.0 0.1 all_to_all.18
  54.1 14.2 %all_gather.12 = bf16[320,1024]{1,0:T(8,128)(2,1)} all-gather(bf16[160,1024]{1,0:T(8,128)(2,1)S(1)} %all_to_all.18), channel_id=1, replica_groups=mesh['dp'=2,'expert'=4,'tile'=4] {'dp'}, dimensions={0}, use_global_device_ids=true | all-gather | bytes 983040 | tf_op jit(solution)/shard_map/all_gather | solution.py:70
  68.3 0.0 all-gather.4.cloned.1.call-update
  68.3 0.0 all-gather.8.cloned.1.call-start
  68.3 0.0 all-gather.6.cloned.1.call-done
  68.4 0.7 all-gather.8.cloned.1.call-update
  69.0 19.6 %psum.7 = f32[4]{0:T(128)S(1)} all-reduce(f32[4]{0:T(128)S(1)} %get-tuple-element.2), channel_id=1, replica_groups=mesh['dp'=2,'expert'=4,'tile'=4] {'dp','expert'}, use_global_device_ids=true, to_apply=%region_4.5 | all-reduce | flops 4 | bytes 32 | tf_op jit(solution)/shard_map/psum | solution.py:63
  88.6 0.6 fusion.16
  89.9 0.0 copy-start.1
  89.9 3.8 %all-gather.4.cloned.1.call-done = bf16[320,4096]{1,0:T(8,128)(2,1)} async-done(((bf16[320,1024]{1,0:T(8,128)(2,1)}), bf16[320,4096]{1,0:T(8,128)(2,1)}) %all-gather.4.cloned.1.call-update) | async-done | bytes 2621456 | tf_op jit(solution)/shard_map/all_gather | solution.py:88
  93.7 7.3 %multiply_bitcast_fusion.1 = f32[1,1024,2048]{2,1,0:T(8,128)} fusion(bf16[320,1024]{1,0:T(8,128)(2,1)} %all_gather.12, f32[]{:T(128)S(6)} %div.27, bf16[320,4096]{1,0:T(8,128)(2,1)} %all-gather.4.cloned.1.call-done, s32[]{:T(128)S(6)} %select_n.54), kind=kOutput, calls=%fused_computation.1 | convolution fusion | flops 1344274432 | bytes 10354696 | tf_op jit(solution)/shard_map/dot_general | solution.py:13
  101.0 31.0 %all-gather.8.cloned.1.call-done = bf16[320,7168]{1,0:T(8,128)(2,1)} async-done(((bf16[320,1792]{1,0:T(8,128)(2,1)}), bf16[320,7168]{1,0:T(8,128)(2,1)}) %all-gather.8.cloned.1.call-update) | async-done | bytes 4587536 | tf_op jit(solution)/shard_map/all_gather | solution.py:89
  132.0 0.0 copy-done.1
  132.0 14.3 %multiply_bitcast_fusion = f32[1,1792,3584]{2,1,0:T(8,128)} fusion(bf16[320,1792]{1,0:T(8,128)(2,1)S(1)} %copy-done.1, f32[]{:T(128)S(6)} %div.27, bf16[320,7168]{1,0:T(8,128)(2,1)} %all-gather.8.cloned.1.call-done, s32[]{:T(128)S(6)} %select_n.58), kind=kOutput, calls=%fused_computation | convolution fusion | flops 4116840448 | bytes 29130760 | tf_op jit(solution)/shard_map/dot_general | solution.py:13
  (5 shorter events, 0.1 us)
Async XLA Ops:
  7.2 31.9 %copy-start = (bf16[64,1024]{1,0:T(8,128)(2,1)S(1)}, bf16[64,1024]{1,0:T(8,128)(2,1)}, u32[]{:S(2)}) copy-start(bf16[64,1024]{1,0:T(8,128)(2,1)} %param.4) | copy-start | bytes 393220
  7.2 12.6 %copy-start.2 = (s32[64,2]{0,1:T(2,128)S(1)}, s32[64,2]{0,1:T(2,128)}, u32[]{:S(2)}) copy-start(s32[64,2]{0,1:T(2,128)} %param.6) | copy-start | bytes 1540
  11.8 26.2 %all-to-all-start.1 = ((bf16[8,20,1792]{2,1,0:T(8,128)(2,1)}), bf16[8,20,1792]{2,1,0:T(8,128)(2,1)S(1)}, u32[]{:S(2)}, u32[]{:S(2)}) async-start(bf16[8,20,1792]{2,1,0:T(8,128)(2,1)} %all_to_all.19), calls=%async_computation.1 | async-start | bytes 1376256 | tf_op jit(solution)/shard_map/all_to_all | solution.py:61
  19.1 49.3 %all-gather.6.cloned.1.call-start = ((), (), s32[]{:S(2)}) async-start(), calls=%async_computation.3 | async-start | bytes 1720320 | tf_op jit(solution)/shard_map/all_gather | solution.py:71
  38.9 54.8 %all-gather.4.cloned.1.call-start = ((), (), s32[]{:S(2)}) async-start(), calls=%async_computation.2 | async-start | bytes 3276800 | tf_op jit(solution)/shard_map/all_gather | solution.py:88
  68.3 63.7 %all-gather.8.cloned.1.call-start = ((), (), s32[]{:S(2)}) async-start(), calls=%async_computation.4 | async-start | bytes 5734400 | tf_op jit(solution)/shard_map/all_gather | solution.py:89
  89.9 42.1 %copy-start.1 = (bf16[320,1792]{1,0:T(8,128)(2,1)S(1)}, bf16[320,1792]{1,0:T(8,128)(2,1)}, u32[]{:S(2)}) copy-start(bf16[320,1792]{1,0:T(8,128)(2,1)} %all-gather.6.cloned.1.call-done) | copy-start | bytes 3440644
Sparse Core Ops, SparseCore 0:
  39.0 28.0 all-gather.5
  68.7 24.9 all-gather.3
  95.3 36.6 all-gather.7
where the time goes:
time: 153 us
  waiting for transfers between devices  53.6 us (35%)
  blocking collectives  48.3 us (32%)
  matrix products  22.1 us (14%)
  between operations  15.3 us (10%)
  starting transfers between devices  7.43 us (5%)
  local copies, waits for them, and re-layouts  4.82 us (3%)
    all_gather x1, waiting for transfers between devices, on_device(): lax.all_gather(all_hidden, 'tile', axis=1, tiled=True)  31 us
    dot_general x2, matrix products, contract(): lax.dot_general(left, right, (((0,), (0,)), ((), ())), preferred_element_...  21.6 us
    psum x1, blocking collectives, on_device(): global_counts = lax.psum(local_counts, ('dp', 'expert'))  19.6 us
    all_to_all x1, waiting for transfers between devices, on_device(): lax.all_to_all(send_hidden, ('dp', 'expert'), split_axis=0, concat_axis=0...  18.1 us
    all_to_all x1, blocking collectives, on_device(): lax.all_to_all(send_tokens, ('dp', 'expert'), split_axis=0, concat_axis=0...  14.5 us
    all_gather x1, blocking collectives, on_device(): lax.all_gather(slot_tokens, 'dp', axis=0, tiled=True)  14.2 us
    all_to_all x1, starting transfers between devices, on_device(): lax.all_to_all(send_hidden, ('dp', 'expert'), split_axis=0, concat_axis=0...  7.31 us
    all_gather x1, waiting for transfers between devices, on_device(): lax.all_gather(all_tokens, 'tile', axis=1, tiled=True)  3.79 us
  transfers between devices with their start and end apart: 4, of which 3 were waited for; matrix products, arithmetic and copies ran while one was open for 6% of the time, Pallas kernels for 0%

commit v1 on v0

--- a/solution.py
+++ b/solution.py
@@ -2,6 +2,12 @@
 import jax.numpy as jnp
 from jax import lax
 from jax.sharding import PartitionSpec as P
+
+
+def heaps_serve(frame):
+    reply = lax.all_gather(frame, "tile")
+    view_out = jnp.concatenate(reply, axis=1)
+    return view_out
 
 
 def broadcast(value, axis, source):
@@ -86,7 +92,7 @@
     else:
         wide_tokens, wide_hidden = (
             lax.all_gather(all_tokens, "tile", axis=1, tiled=True),
-            lax.all_gather(all_hidden, "tile", axis=1, tiled=True),
+            heaps_serve(all_hidden),
         )
         column_tokens = lax.dynamic_slice_in_dim(
             wide_tokens, group_index * width_tokens, width_tokens, 1

time: 153 us -> 159 us (1.039)
  local copies, waits for them, and re-layouts: 4.82 us -> 11.9 us
  matrix products: 22.1 us -> 20.5 us
    all_gather x0 -> x1, local copies, waits for them, and re-layouts: none -> 5.84 us  [heaps_serve(): reply = lax.all_gather(frame, 'tile')]
    dot_general x2, matrix products: 21.6 us -> 19.9 us  [contract(): lax.dot_general(left, right, (((0,), (0,)), ((), ())), preferred_element_...]
where the time goes in v1:
time: 159 us; the launch traced here: 158 us
  waiting for transfers between devices  53.4 us (34%)
  blocking collectives  48.5 us (31%)
  matrix products  20.5 us (13%)
  between operations  15.3 us (10%)
  local copies, waits for them, and re-layouts  11.9 us (7%)
  starting transfers between devices  7.43 us (5%)
    all_gather x1, waiting for transfers between devices, heaps_serve(): reply = lax.all_gather(frame, 'tile')  31 us
    dot_general x2, matrix products, contract(): lax.dot_general(left, right, (((0,), (0,)), ((), ())), preferred_element_...  19.9 us
    psum x1, blocking collectives, on_device(): global_counts = lax.psum(local_counts, ('dp', 'expert'))  19.8 us
    all_to_all x1, waiting for transfers between devices, on_device(): lax.all_to_all(send_hidden, ('dp', 'expert'), split_axis=0, concat_axis=0...  18.1 us
    all_to_all x1, blocking collectives, on_device(): lax.all_to_all(send_tokens, ('dp', 'expert'), split_axis=0, concat_axis=0...  14.5 us
    all_gather x1, blocking collectives, on_device(): lax.all_gather(slot_tokens, 'dp', axis=0, tiled=True)  14.2 us
    all_to_all x1, starting transfers between devices, on_device(): lax.all_to_all(send_hidden, ('dp', 'expert'), split_axis=0, concat_axis=0...  7.31 us
    all_gather x1, local copies, waits for them, and re-layouts, heaps_serve(): reply = lax.all_gather(frame, 'tile')  5.84 us
  transfers between devices with their start and end apart: 4, of which 3 were waited for; matrix products, arithmetic and copies ran while one was open for 6% of the time, Pallas kernels for 0%

profile of v1, /device:TPU:0, one launch (start us, length us, event | category | flops | bytes accessed | tf_op | source)
XLA Modules:
  0.0 158.2 jit_solution(8036466624012088871)
XLA Ops:
  7.2 0.0 copy-start
  7.2 0.0 copy-start.2
  7.9 0.8 copy.22
  8.7 0.1 eq.43
  8.8 0.1 fusion.5
  8.9 0.2 reduce_window_sum.11
  9.1 0.2 fusion.6
  9.3 1.2 reshape.96
  10.5 0.3 convolution_convert_fusion
  10.8 1.0 all_to_all.19
  11.8 7.3 %all-to-all-start.1 = ((bf16[8,20,1792]{2,1,0:T(8,128)(2,1)}), bf16[8,20,1792]{2,1,0:T(8,128)(2,1)S(1)}, u32[]{:S(2)}, u32[]{:S(2)}) async-start(bf16[8,20,1792]{2,1,0:T(8,128)(2,1)} %all_to_all.19), calls=%async_computation.1 | async-start | bytes 1376256 | tf_op jit(solution)/shard_map/all_to_all | solution.py:67
  19.1 0.0 all-gather.7.cloned.1.call-start
  19.1 0.1 ne.82
  19.3 0.1 copy.24
  19.4 0.1 div.25
  19.5 0.1 copy.25
  19.6 0.1 rem.32
  19.8 0.1 copy.23
  19.8 0.0 copy-done.2
  19.9 18.1 %all-to-all-done.1 = bf16[8,20,1792]{2,1,0:T(8,128)(2,1)S(1)} async-done(((bf16[8,20,1792]{2,1,0:T(8,128)(2,1)}), bf16[8,20,1792]{2,1,0:T(8,128)(2,1)S(1)}, u32[]{:S(2)}, u32[]{:S(2)}) %all-to-all-start.1) | async-done | bytes 573472 | tf_op jit(solution)/shard_map/all_to_all | solution.py:67
  38.0 0.9 all_to_all.21
  38.9 0.0 all-gather.7.cloned.1.call-update
  38.9 0.0 all-gather.5.cloned.1.call-start
  39.0 0.1 convert_reduce_fusion
  39.1 0.0 copy-done
  39.1 0.3 convolution_convert_fusion.1
  39.4 0.1 all_to_all.16
  39.5 14.5 %all_to_all.24 = bf16[8,20,1024]{2,1,0:T(8,128)(2,1)S(1)} all-to-all(bf16[8,20,1024]{2,1,0:T(8,128)(2,1)S(1)} %all_to_all.16), channel_id=1, replica_groups=mesh['dp'=2,'expert'=4,'tile'=4] {'dp','expert'}, dimensions={0} | all-to-all | bytes 655360 | tf_op jit(solution)/shard_map/all_to_all | solution.py:66
  54.0 0.1 all_to_all.18
  54.1 14.2 %all_gather.15 = bf16[320,1024]{1,0:T(8,128)(2,1)} all-gather(bf16[160,1024]{1,0:T(8,128)(2,1)S(1)} %all_to_all.18), channel_id=1, replica_groups=mesh['dp'=2,'expert'=4,'tile'=4] {'dp'}, dimensions={0}, use_global_device_ids=true | all-gather | bytes 983040 | tf_op jit(solution)/shard_map/all_gather | solution.py:76
  68.3 0.0 all-gather.5.cloned.1.call-update
  68.3 0.0 all-gather.9.cloned.1.call-start
  68.3 0.0 all-gather.7.cloned.1.call-done
  68.4 0.7 all-gather.9.cloned.1.call-update
  69.0 19.8 %psum.7 = f32[4]{0:T(128)S(1)} all-reduce(f32[4]{0:T(128)S(1)} %get-tuple-element.2), channel_id=1, replica_groups=mesh['dp'=2,'expert'=4,'tile'=4] {'dp','expert'}, use_global_device_ids=true, to_apply=%region_4.5 | all-reduce | flops 4 | bytes 32 | tf_op jit(solution)/shard_map/psum | solution.py:69
  88.8 0.6 fusion.16
  90.1 3.6 %all-gather.5.cloned.1.call-done = bf16[320,4096]{1,0:T(8,128)(2,1)} async-done(((bf16[320,1024]{1,0:T(8,128)(2,1)}), bf16[320,4096]{1,0:T(8,128)(2,1)}) %all-gather.5.cloned.1.call-update) | async-done | bytes 2621456 | tf_op jit(solution)/shard_map/all_gather | solution.py:94
  93.7 7.3 %multiply_bitcast_fusion.1 = f32[1,1024,2048]{2,1,0:T(8,128)} fusion(bf16[320,1024]{1,0:T(8,128)(2,1)} %all_gather.15, f32[]{:T(128)S(6)} %div.27, bf16[320,4096]{1,0:T(8,128)(2,1)} %all-gather.5.cloned.1.call-done, s32[]{:T(128)S(6)} %select_n.54), kind=kOutput, calls=%fused_computation.1 | convolution fusion | flops 1344274432 | bytes 10354696 | tf_op jit(solution)/shard_map/dot_general | solution.py:19
  101.0 31.0 %all-gather.9.cloned.1.call-done = bf16[1280,1792]{1,0:T(8,128)(2,1)} async-done(((bf16[320,1792]{1,0:T(8,128)(2,1)}), bf16[1280,1792]{1,0:T(8,128)(2,1)}) %all-gather.9.cloned.1.call-update) | async-done | bytes 4587536 | tf_op jit(solution)/shard_map/all_gather | solution.py:8
  132.0 5.8 %copy.30 = bf16[4,320,1792]{2,0,1:T(4,128)(2,1)S(1)} copy(bf16[4,320,1792]{2,1,0:T(8,128)(2,1)} %bitcast.18) | data formatting | bytes 9175040 | tf_op jit(solution)/shard_map/all_gather | solution.py:8
  137.8 0.0 copy-start.1
  137.8 0.9 copy.31
  138.7 0.3 copy-done.1
  139.1 12.6 %multiply_bitcast_fusion = f32[1,1792,3584]{2,1,0:T(8,128)} fusion(bf16[320,1792]{1,0:T(8,128)(2,1)S(1)} %copy-done.1, f32[]{:T(128)S(6)} %div.27, bf16[320,7168]{1,0:T(8,128)(2,1)S(1)} %bitcast.17, s32[]{:T(128)S(6)} %select_n.58), kind=kOutput, calls=%fused_computation | convolution fusion | flops 4116840448 | bytes 29130760 | tf_op jit(solution)/shard_map/dot_general | solution.py:19
  (5 shorter events, 0.1 us)
Async XLA Ops:
  7.2 31.9 %copy-start = (bf16[64,1024]{1,0:T(8,128)(2,1)S(1)}, bf16[64,1024]{1,0:T(8,128)(2,1)}, u32[]{:S(2)}) copy-start(bf16[64,1024]{1,0:T(8,128)(2,1)} %param.4) | copy-start | bytes 393220
  7.2 12.6 %copy-start.2 = (s32[64,2]{0,1:T(2,128)S(1)}, s32[64,2]{0,1:T(2,128)}, u32[]{:S(2)}) copy-start(s32[64,2]{0,1:T(2,128)} %param.6) | copy-start | bytes 1540
  11.8 26.2 %all-to-all-start.1 = ((bf16[8,20,1792]{2,1,0:T(8,128)(2,1)}), bf16[8,20,1792]{2,1,0:T(8,128)(2,1)S(1)}, u32[]{:S(2)}, u32[]{:S(2)}) async-start(bf16[8,20,1792]{2,1,0:T(8,128)(2,1)} %all_to_all.19), calls=%async_computation.1 | async-start | bytes 1376256 | tf_op jit(solution)/shard_map/all_to_all | solution.py:67
  19.1 49.3 %all-gather.7.cloned.1.call-start = ((), (), s32[]{:S(2)}) async-start(), calls=%async_computation.3 | async-start | bytes 1720320 | tf_op jit(solution)/shard_map/all_gather | solution.py:77
  38.9 54.7 %all-gather.5.cloned.1.call-start = ((), (), s32[]{:S(2)}) async-start(), calls=%async_computation.2 | async-start | bytes 3276800 | tf_op jit(solution)/shard_map/all_gather | solution.py:94
  68.3 63.7 %all-gather.9.cloned.1.call-start = ((), (), s32[]{:S(2)}) async-start(), calls=%async_computation.4 | async-start | bytes 5734400 | tf_op jit(solution)/shard_map/all_gather | solution.py:8
  137.8 1.3 copy-start.1
Sparse Core Ops, SparseCore 0:
  39.0 28.0 all-gather.6
  68.7 24.8 all-gather.4
  95.2 36.6 all-gather.8
